TPU v7x, 32 devices: a whole 2x2x4 slice. The times are simulated.
32 devices in a mesh: seq: 8 (over z, core), fsdp: 4 (over y, x).
Axes of the slice: x: 2, y: 2, z: 4, core: 2. Of those that a mesh axis runs over, the one named last changes fastest.
Arguments:
- tokens: bfloat16 [4, 1024, 2048], P('fsdp', 'seq'), may hold values from -6 to 6
- ln_gain: bfloat16 [2048], P('fsdp'), may hold values from 0.5 to 1.5
- ln_bias: bfloat16 [2048], P('fsdp'), may hold values from -3 to 3
- qkv_weight: bfloat16 [2048, 6144], P('fsdp')
- qkv_bias: bfloat16 [6144], P('fsdp'), may hold values from -3 to 3
- dense_weight: bfloat16 [2048, 2048], P('fsdp'), may hold values from -0.5 to 0.5
- dense_bias: bfloat16 [2048], P('fsdp'), may hold values from -3 to 3
- fc1_weight: bfloat16 [2048, 8192], P('fsdp'), may hold values from -0.125 to 0.125
- fc1_bias: bfloat16 [8192], P('fsdp'), may hold values from -3 to 3
- fc2_weight: bfloat16 [8192, 2048], P('fsdp'), may hold values from -0.0625 to 0.0625
- fc2_bias: bfloat16 [2048], P('fsdp'), may hold values from -3 to 3
- segments: int32 [4, 1024], P('fsdp'), may hold values from 0 to 1, as said below
- positions: int32 [4, 1024], P('fsdp', 'seq'), may hold values from 0 to 2046, as said below
- cotangent: bfloat16 [4, 1024, 2048], P('fsdp', 'seq'), may hold values from -6 to 6
Outputs:
- out: bfloat16 [4, 1024, 2048], P('fsdp', 'seq')
- grad_tokens: float32 [4, 1024, 2048], P('fsdp', 'seq')
- grad_ln_gain: float32 [2048], P('fsdp')
- grad_ln_bias: float32 [2048], P('fsdp')
- grad_qkv_weight: float32 [2048, 6144], P('fsdp')
- grad_qkv_bias: float32 [6144], P('fsdp')
- grad_dense_weight: float32 [2048, 2048], P('fsdp')
- grad_dense_bias: float32 [2048], P('fsdp')
- grad_fc1_weight: float32 [2048, 8192], P('fsdp')
- grad_fc1_bias: float32 [8192], P('fsdp')
- grad_fc2_weight: float32 [8192, 2048], P('fsdp')
- grad_fc2_bias: float32 [2048], P('fsdp')
Inputs may be any that keep to these rules, and one draw needn't show every extreme that they name: `segments`: document numbers never fall along a sequence and each of 0 to 1 occurs in every sequence. The first document of each sequence starts at position 0; positions rise by one from token to token within a document; in every sequence the last token of the last document has position 2046.
All inputs are finite; a program needn't handle non-finite values.
Results may differ from a plain program's by a relative error of at most 0.0095.
Values may be sent and summed in bfloat16 or wider, within the bound.
A program may use at most 448 MiB of HBM per device.

v0:
```python
import jax
import jax.numpy as jnp
from jax import lax
from jax.sharding import PartitionSpec as P

HEADS = 32
HEAD = 64
ROT = 32
norm_epsilon = 1e-05


def rotary_angles(pos_row, rot_width):
    inverse = 1.0 / 10000.0 ** (jnp.arange(0, rot_width, 2, dtype=jnp.float32) / rot_width)
    return pos_row.astype(jnp.float32)[:, None] * inverse[None, :]


def rotate_pair(values_in, angles):
    half_width = angles.shape[-1]
    cosine = jnp.cos(angles)[:, None, None, :]
    sine_part = jnp.sin(angles)[:, None, None, :]
    low_half = values_in[..., :half_width]
    high_half = values_in[..., half_width : 2 * half_width]
    rest_part = values_in[..., 2 * half_width :]
    return jnp.concatenate(
        [
            low_half * cosine - high_half * sine_part,
            high_half * cosine + low_half * sine_part,
            rest_part,
        ],
        axis=-1,
    )


def gelu_tanh(values_in):
    return jax.nn.gelu(values_in, approximate=True)


def contract_rows(left_side, right_side):
    return lax.dot_general(
        left_side, right_side, (((0,), (0,)), ((), ())), preferred_element_type=jnp.float32
    )


def contract_cols(left_side, right_side):
    return lax.dot_general(
        left_side, right_side, (((1,), (1,)), ((), ())), preferred_element_type=jnp.float32
    )


def block_scores(query_block, keys_all, first_row, seg_row):
    block_len = query_block.shape[0]
    seq_len = keys_all.shape[0]
    score_scale = query_block.shape[2] ** (-0.5)
    scores = (
        jnp.einsum("qhd,khd->hqk", query_block, keys_all, preferred_element_type=jnp.float32)
        * score_scale
    )
    query_place = first_row + jnp.arange(block_len)
    key_place = jnp.arange(seq_len)
    query_seg = lax.dynamic_slice_in_dim(seg_row, first_row, block_len, 0)
    allowed = (key_place[None, :] <= query_place[:, None]) & (
        query_seg[:, None] == seg_row[None, :]
    )
    return (jnp.where(allowed[None], scores, -1e30), allowed)


def attend_forward(queries, keys_all, values, seg_row):
    seq_len = queries.shape[0]
    block_len = min(512, seq_len)
    count_blocks = seq_len // block_len

    def one_block(block_index):
        first_row = block_index * block_len
        query_block = lax.dynamic_slice_in_dim(queries, first_row, block_len, 0)
        scores, allowed = block_scores(query_block, keys_all, first_row, seg_row)
        row_top = jnp.max(scores, axis=-1, keepdims=True)
        raised = jnp.exp(scores - row_top)
        row_total = jnp.sum(raised, axis=-1, keepdims=True)
        probabilities = raised / row_total
        result = jnp.einsum(
            "hqk,khd->qhd",
            probabilities.astype(jnp.bfloat16),
            values,
            preferred_element_type=jnp.float32,
        )
        return (result, row_top[..., 0] + jnp.log(row_total[..., 0]))

    outputs, log_norm = lax.map(one_block, jnp.arange(count_blocks))
    return (outputs.reshape(seq_len, queries.shape[1], queries.shape[2]), log_norm)


def attend_backward(queries, keys_all, values, seg_row, log_norm, grad_out):
    seq_len = queries.shape[0]
    block_len = min(512, seq_len)
    count_blocks = seq_len // block_len
    score_scale = queries.shape[2] ** (-0.5)

    def one_block(running, block_index):
        grad_keys, grad_values = running
        first_row = block_index * block_len
        query_block = lax.dynamic_slice_in_dim(queries, first_row, block_len, 0)
        grad_block = lax.dynamic_slice_in_dim(grad_out, first_row, block_len, 0)
        scores, allowed = block_scores(query_block, keys_all, first_row, seg_row)
        probabilities = jnp.where(
            allowed[None], jnp.exp(scores - log_norm[block_index][..., None]), 0.0
        )
        grad_probs = jnp.einsum(
            "qhd,khd->hqk", grad_block, values, preferred_element_type=jnp.float32
        )
        row_inner = jnp.sum(probabilities * grad_probs, axis=-1, keepdims=True)
        grad_scores = (probabilities * (grad_probs - row_inner)).astype(jnp.bfloat16)
        grad_query = (
            jnp.einsum("hqk,khd->qhd", grad_scores, keys_all, preferred_element_type=jnp.float32)
            * score_scale
        )
        grad_keys = (
            grad_keys
            + jnp.einsum(
                "hqk,qhd->khd", grad_scores, query_block, preferred_element_type=jnp.float32
            )
            * score_scale
        )
        grad_values = grad_values + jnp.einsum(
            "hqk,qhd->khd",
            probabilities.astype(jnp.bfloat16),
            grad_block,
            preferred_element_type=jnp.float32,
        )
        return ((grad_keys, grad_values), grad_query)

    zeros_start = jnp.zeros(keys_all.shape, jnp.float32)
    (grad_keys, grad_values), grad_queries = lax.scan(
        one_block, (zeros_start, zeros_start), jnp.arange(count_blocks)
    )
    return (grad_queries.reshape(queries.shape), grad_keys, grad_values)


def body(
    tokens,
    ln_gain,
    ln_bias,
    qkv_weight,
    qkv_bias,
    dense_weight,
    dense_bias,
    fc1_weight,
    fc1_bias,
    fc2_weight,
    fc2_bias,
    segments,
    positions,
    cotangent,
):
    seq_count = lax.axis_size("seq")
    shard_count = lax.axis_size("fsdp")
    gathered = (
        lax.all_gather(qkv_weight, "fsdp", axis=0, tiled=True),
        lax.all_gather(dense_weight, "fsdp", axis=0, tiled=True),
        lax.all_gather(fc1_weight, "fsdp", axis=0, tiled=True),
        lax.all_gather(fc2_weight, "fsdp", axis=0, tiled=True),
        lax.all_gather(ln_gain, "fsdp", axis=0, tiled=True),
        lax.all_gather(ln_bias, "fsdp", axis=0, tiled=True),
        lax.all_gather(qkv_bias, "fsdp", axis=0, tiled=True),
        lax.all_gather(dense_bias, "fsdp", axis=0, tiled=True),
        lax.all_gather(fc1_bias, "fsdp", axis=0, tiled=True),
        lax.all_gather(fc2_bias, "fsdp", axis=0, tiled=True),
    )
    w_qkv, w_dense, w_up, w_down = (gathered[0], gathered[1], gathered[2], gathered[3])
    gain_full, shift_full, b_qkv, b_dense, b_up, b_down = (
        gathered[4],
        gathered[5],
        gathered[6],
        gathered[7],
        gathered[8],
        gathered[9],
    )
    tok_len = tokens.shape[1]
    model_width = tokens.shape[2]
    heads_here = HEADS // seq_count
    head_slab = heads_here * HEAD
    inputs = tokens[0].astype(jnp.float32)
    centre = jnp.mean(inputs, axis=-1, keepdims=True)
    variance = jnp.mean((inputs - centre) ** 2, axis=-1, keepdims=True)
    inv_std = lax.rsqrt(variance + norm_epsilon)
    standard = (inputs - centre) * inv_std
    normed = (standard * gain_full.astype(jnp.float32) + shift_full.astype(jnp.float32)).astype(
        jnp.bfloat16
    )
    projected = jnp.dot(normed, w_qkv, preferred_element_type=jnp.float32) + b_qkv.astype(
        jnp.float32
    )
    projected = projected.reshape(tok_len, 3, HEADS, HEAD)
    angles = rotary_angles(positions[0], ROT)
    turned = jnp.concatenate(
        [rotate_pair(projected[:, :2], angles), projected[:, 2:]], axis=1
    ).astype(jnp.bfloat16)
    outgoing = turned.reshape(tok_len, 3, seq_count, head_slab)
    by_heads = lax.all_to_all(outgoing, "seq", split_axis=2, concat_axis=0, tiled=True)
    seq_len = by_heads.shape[0]
    by_heads = by_heads.reshape(seq_len, 3, heads_here, HEAD)
    queries, keys_all, values = (by_heads[:, 0], by_heads[:, 1], by_heads[:, 2])
    seg_row = segments[0]
    attended, log_norm = attend_forward(queries, keys_all, values, seg_row)
    returned_heads = lax.all_to_all(
        attended.astype(jnp.bfloat16).reshape(seq_len, 1, head_slab),
        "seq",
        split_axis=0,
        concat_axis=1,
        tiled=True,
    )
    att_tokens = returned_heads.reshape(tok_len, model_width)
    branch_att = jnp.dot(att_tokens, w_dense, preferred_element_type=jnp.float32) + b_dense.astype(
        jnp.float32
    )
    pre_act = jnp.dot(normed, w_up, preferred_element_type=jnp.float32) + b_up.astype(jnp.float32)
    activated = gelu_tanh(pre_act).astype(jnp.bfloat16)
    branch_mlp = jnp.dot(activated, w_down, preferred_element_type=jnp.float32) + b_down.astype(
        jnp.float32
    )
    result = (inputs + branch_att + branch_mlp).astype(jnp.bfloat16)
    regathered = (
        lax.all_gather(qkv_weight, "fsdp", axis=0, tiled=True),
        lax.all_gather(dense_weight, "fsdp", axis=0, tiled=True),
        lax.all_gather(fc1_weight, "fsdp", axis=0, tiled=True),
        lax.all_gather(fc2_weight, "fsdp", axis=0, tiled=True),
        lax.all_gather(ln_gain, "fsdp", axis=0, tiled=True),
        lax.all_gather(ln_bias, "fsdp", axis=0, tiled=True),
        lax.all_gather(qkv_bias, "fsdp", axis=0, tiled=True),
        lax.all_gather(dense_bias, "fsdp", axis=0, tiled=True),
        lax.all_gather(fc1_bias, "fsdp", axis=0, tiled=True),
        lax.all_gather(fc2_bias, "fsdp", axis=0, tiled=True),
    )
    w_qkv, w_dense, w_up, w_down = (regathered[0], regathered[1], regathered[2], regathered[3])
    gain_full = regathered[4]
    upstream = cotangent[0]
    grad_act = contract_cols(upstream, w_down)
    grad_slope = jax.vjp(gelu_tanh, pre_act)[1](grad_act)[0]
    grad_pre = grad_slope.astype(jnp.bfloat16)
    grad_att = contract_cols(upstream, w_dense).astype(jnp.bfloat16)
    heads_grad = lax.all_to_all(
        grad_att.reshape(tok_len, seq_count, head_slab),
        "seq",
        split_axis=1,
        concat_axis=0,
        tiled=True,
    )
    heads_grad = heads_grad.reshape(seq_len, heads_here, HEAD)
    grad_q, grad_k, grad_v = attend_backward(
        queries, keys_all, values, seg_row, log_norm, heads_grad
    )
    stacked = (
        jnp.stack([grad_q, grad_k, grad_v], axis=1)
        .astype(jnp.bfloat16)
        .reshape(seq_len, 3, 1, head_slab)
    )
    returned = lax.all_to_all(stacked, "seq", split_axis=0, concat_axis=2, tiled=True)
    returned = returned.reshape(tok_len, 3, HEADS, HEAD).astype(jnp.float32)
    unturned = jnp.concatenate([rotate_pair(returned[:, :2], -angles), returned[:, 2:]], axis=1)
    grad_mixed = unturned.reshape(tok_len, 3 * model_width).astype(jnp.bfloat16)
    grad_normed = contract_cols(grad_mixed, w_qkv) + contract_cols(grad_pre, w_up)
    scaled = grad_normed * gain_full.astype(jnp.float32)
    grad_inputs = upstream.astype(jnp.float32) + inv_std * (
        scaled
        - jnp.mean(scaled, axis=-1, keepdims=True)
        - standard * jnp.mean(scaled * standard, axis=-1, keepdims=True)
    )
    gain_term = jnp.sum(grad_normed * standard, axis=0)
    shift_term = jnp.sum(grad_normed, axis=0)
    qkv_term = jnp.sum(grad_mixed.astype(jnp.float32), axis=0)
    out_term = jnp.sum(upstream.astype(jnp.float32), axis=0)
    up_term = jnp.sum(grad_pre.astype(jnp.float32), axis=0)

    def spread_vec(vector):
        return vector.reshape(shard_count, seq_count, -1).transpose(1, 0, 2).reshape(-1)

    vector_parts = (
        lax.psum_scatter(spread_vec(gain_term), ("seq", "fsdp"), scatter_dimension=0, tiled=True),
        lax.psum_scatter(spread_vec(shift_term), ("seq", "fsdp"), scatter_dimension=0, tiled=True),
        lax.psum_scatter(spread_vec(qkv_term), ("seq", "fsdp"), scatter_dimension=0, tiled=True),
        lax.psum_scatter(spread_vec(out_term), ("seq", "fsdp"), scatter_dimension=0, tiled=True),
        lax.psum_scatter(spread_vec(up_term), ("seq", "fsdp"), scatter_dimension=0, tiled=True),
    )
    ff_width = w_up.shape[1]
    col_qkv = 3 * model_width // seq_count
    col_up = ff_width // seq_count
    row_dense = model_width // (shard_count * seq_count)
    row_down = ff_width // (shard_count * seq_count)
    normed_full, upstream_full = (
        lax.all_gather(normed, "seq", axis=0, tiled=True),
        lax.all_gather(upstream, "seq", axis=0, tiled=True),
    )
    grads_cols = (
        lax.all_to_all(
            grad_mixed.reshape(tok_len, seq_count, col_qkv),
            "seq",
            split_axis=1,
            concat_axis=0,
            tiled=True,
        ),
        lax.all_to_all(
            grad_pre.reshape(tok_len, seq_count, col_up),
            "seq",
            split_axis=1,
            concat_axis=0,
            tiled=True,
        ),
    )
    mixed_cols = grads_cols[0].reshape(seq_len, col_qkv)
    pre_cols = grads_cols[1].reshape(seq_len, col_up)
    rows_sel = (
        lax.all_to_all(
            att_tokens.reshape(tok_len, shard_count, seq_count, row_dense),
            "seq",
            split_axis=2,
            concat_axis=0,
            tiled=True,
        ),
        lax.all_to_all(
            activated.reshape(tok_len, shard_count, seq_count, row_down),
            "seq",
            split_axis=2,
            concat_axis=0,
            tiled=True,
        ),
    )
    att_sel = rows_sel[0].reshape(seq_len, shard_count * row_dense)
    down_sel = rows_sel[1].reshape(seq_len, shard_count * row_down)

    def moved_sum(left_full, right_side):
        return lax.psum_scatter(
            contract_rows(left_full, right_side).astype(jnp.bfloat16),
            "fsdp",
            scatter_dimension=0,
            tiled=True,
        ).astype(jnp.float32)

    piece_qkv = moved_sum(normed_full, mixed_cols)
    piece_dense = moved_sum(att_sel, upstream_full)
    piece_up = moved_sum(normed_full, pre_cols)
    piece_down = moved_sum(down_sel, upstream_full)
    reduced = (
        lax.all_gather(piece_qkv.astype(jnp.bfloat16), "seq", axis=1, tiled=True).astype(
            piece_qkv.dtype
        ),
        lax.all_gather(piece_dense.astype(jnp.bfloat16), "seq", axis=0, tiled=True).astype(
            piece_dense.dtype
        ),
        lax.all_gather(piece_up.astype(jnp.bfloat16), "seq", axis=1, tiled=True).astype(
            piece_up.dtype
        ),
        lax.all_gather(piece_down.astype(jnp.bfloat16), "seq", axis=0, tiled=True).astype(
            piece_down.dtype
        ),
        lax.all_gather(vector_parts[0].astype(jnp.bfloat16), "seq", axis=0, tiled=True).astype(
            jnp.float32
        ),
        lax.all_gather(vector_parts[1].astype(jnp.bfloat16), "seq", axis=0, tiled=True).astype(
            jnp.float32
        ),
        lax.all_gather(vector_parts[2].astype(jnp.bfloat16), "seq", axis=0, tiled=True).astype(
            jnp.float32
        ),
        lax.all_gather(vector_parts[3].astype(jnp.bfloat16), "seq", axis=0, tiled=True).astype(
            jnp.float32
        ),
        lax.all_gather(vector_parts[4].astype(jnp.bfloat16), "seq", axis=0, tiled=True).astype(
            jnp.float32
        ),
    )
    return (
        result[None],
        grad_inputs[None],
        reduced[4],
        reduced[5],
        reduced[0],
        reduced[6],
        reduced[1],
        reduced[7],
        reduced[2],
        reduced[8],
        reduced[3],
        reduced[7],
    )


def solution(mesh):
    return jax.shard_map(
        body,
        mesh=mesh,
        in_specs=(
            P("fsdp", "seq", None),
            P("fsdp"),
            P("fsdp"),
            P("fsdp", None),
            P("fsdp"),
            P("fsdp", None),
            P("fsdp"),
            P("fsdp", None),
            P("fsdp"),
            P("fsdp", None),
            P("fsdp"),
            P("fsdp", None),
            P("fsdp", "seq"),
            P("fsdp", "seq", None),
        ),
        out_specs=(
            P("fsdp", "seq", None),
            P("fsdp", "seq", None),
            P("fsdp"),
            P("fsdp"),
            P("fsdp", None),
            P("fsdp"),
            P("fsdp", None),
            P("fsdp"),
            P("fsdp", None),
            P("fsdp"),
            P("fsdp", None),
            P("fsdp"),
        ),
        check_vma=False,
    )
```

profile of v0, /device:TPU:0, one launch (start us, length us, event | category | flops | bytes accessed | tf_op | source)
XLA Modules:
  0.0 1528.9 jit_solution(6657508894019280868)
XLA Ops:
  9.5 9.6 all-gather.1
  19.1 8.2 all-gather.2
  30.9 7.7 all-gather.3
  39.4 60.9 %all-gather.20.cloned.1.call-done = bf16[2048,2048]{1,0:T(8,128)(2,1)} async-done(((bf16[512,2048]{1,0:T(8,128)(2,1)}), bf16[2048,2048]{1,0:T(8,128)(2,1)}) %all-gather.20.cloned.1.call-update) | async-done | bytes 8388624 | tf_op jit(solution)/shard_map/all_gather | solution.py:158
  112.0 217.8 %all-gather.18.cloned.1.call-done = bf16[2048,6144]{1,0:T(8,128)(2,1)} async-done(((bf16[512,6144]{1,0:T(8,128)(2,1)}), bf16[2048,6144]{1,0:T(8,128)(2,1)}) %all-gather.18.cloned.1.call-update) | async-done | bytes 25165840 | tf_op jit(solution)/shard_map/all_gather | solution.py:157
  329.8 13.3 convolution_add_fusion.1
  354.1 56.5 %all-to-all-done = bf16[128,3,8,256]{0,3,1,2:T(8,128)(2,1)} async-done(((bf16[128,3,8,256]{0,3,1,2:T(8,128)(2,1)}), bf16[128,3,8,256]{0,3,1,2:T(8,128)(2,1)}, u32[]{:S(2)}, u32[]{:S(2)}) %all-to-all-start) | async-done | bytes 1572896 | tf_op jit(solution)/shard_map/all_to_all | solution.py:198
  421.2 20.8 %while.27 = (s32[]{:T(128)}, bf16[2,512,4,64]{1,3,2,0:T(8,128)(2,1)}, f32[2,4,512]{2,1,0:T(4,128)S(1)}, s32[2]{0:T(128)S(1)}, s32[1024]{0:T(1024)S(1)}, /*index=...) while((s32[]{:T(128)}, ...), condition=%wide.region_5.6_spmd, body=%wide.region_2.5_spmd.sunk | while | flops 563608064 | bytes 31275748 | solution.py:88
  462.7 61.2 %while.28 = (s32[]{:T(128)}, f32[1024,4,64]{0,2,1:T(8,128)S(1)}, f32[1024,4,64]{0,2,1:T(8,128)S(1)}, bf16[2,512,4,64]{1,3,2,0:T(8,128)(2,1)}, s32[2]{0:T(128)S(1...) while((s32[]{:T(128)}, f32[1024,4,64]{0,2,1:T(8,128)S(1)}, ...), condition=%wide.region_8.9_spmd.clone, body=%wide.region_6.8_spmd.clone.sunk | while | flops 1366161920 | bytes 180411312 | solution.py:132
  474.0 7.5 multiply_reduce_fusion.3
  539.1 43.7 %all-to-all-done.3 = bf16[1024,3,1,256]{3,1,2,0:T(4,128)(2,1)S(1)} async-done(((bf16[1024,3,1,256]{3,1,2,0:T(4,128)(2,1)}), bf16[1024,3,1,256]{3,1,2,0:T(4,128)(2,1)S(1)}, u32[]{:S(2)}, u32[]{:S(2)}) %all-to-all-start.3) | async-done | bytes 1572896 | tf_op jit(solution)/shard_map/all_to_all | solution.py:256
  612.0 8.7 all_gather.75
  620.7 22.9 %all-to-all-done.4 = bf16[128,8,768]{0,2,1:T(8,128)(2,1)S(1)} async-done(((bf16[128,8,768]{0,2,1:T(8,128)(2,1)}), bf16[128,8,768]{0,2,1:T(8,128)(2,1)S(1)}, u32[]{:S(2)}, u32[]{:S(2)}) %all-to-all-start.4) | async-done | bytes 1572896 | tf_op jit(solution)/shard_map/all_to_all | solution.py:293
  651.9 99.4 %all-gather.22.cloned.1.call-done = bf16[2048,8192]{1,0:T(8,128)(2,1)} async-done(((bf16[512,8192]{1,0:T(8,128)(2,1)}), bf16[2048,8192]{1,0:T(8,128)(2,1)}) %all-gather.22.cloned.1.call-update) | async-done | bytes 33554448 | tf_op jit(solution)/shard_map/all_gather | solution.py:159
  751.3 19.0 %multiply_convert_fusion.1 = (bf16[128,8192]{1,0:T(8,128)(2,1)}, f32[128,8192]{1,0:T(8,128)}) fusion(f32[8192]{0:T(1024)S(1)} %convert_element_type.189, bf16[128,2048]{1,0:T(8,128)(2,1)S(1)} %copy-done.10, bf16[2048,8192]{1,0:T(8,128)(2,1)} %all-gather.22.cloned.1.call-done), kind=kOutput, calls=%fused_computation.59 | convolution fusion | flops 4305453056 | bytes 40402944 | tf_op jit(solution)/shard_map/dot_general | solution.py:215
  770.3 279.8 %all-gather.24.cloned.1.call-done = bf16[8192,2048]{1,0:T(8,128)(2,1)} async-done(((bf16[2048,2048]{1,0:T(8,128)(2,1)}), bf16[8192,2048]{1,0:T(8,128)(2,1)}) %all-gather.24.cloned.1.call-update) | async-done | bytes 33554448 | tf_op jit(solution)/shard_map/all_gather | solution.py:160
  1050.1 18.0 %convert_reduce_fusion = (f32[8192]{0:T(1024)S(1)}, bf16[128,8192]{1,0:T(8,128)(2,1)S(1)}) fusion(f32[128,8192]{1,0:T(8,128)} %get-tuple-element.255, bf16[8192,2048]{1,0:T(8,128)(2,1)} %all-gather.24.cloned.1.call-done, bf16[1,128,2048]{2,1,0:T(8,128)(2,1)S(1)} %copy-done.12), kind=kOutput, calls=%fused_computation.58 | convolution fusion | flops 4318027776 | bytes 40402944 | tf_op jit(solution)/shard_map/dot_general | solution.py:45
  1068.3 53.7 %all_to_all.114 = bf16[128,8,1024]{2,0,1:T(8,128)(2,1)S(1)} all-to-all(bf16[128,8,1024]{2,0,1:T(8,128)(2,1)S(1)} %bitcast.256), channel_id=1, replica_groups=mesh['seq'=8,'fsdp'=4] {'seq'}, dimensions={1} | all-to-all | bytes 4194304 | tf_op jit(solution)/shard_map/all_to_all | solution.py:300
  1136.4 53.1 %all_to_all.115 = bf16[128,4,8,256]{0,3,1,2:T(8,128)(2,1)S(1)} all-to-all(bf16[128,4,8,256]{0,3,1,2:T(8,128)(2,1)} %copy.127), channel_id=1, replica_groups=mesh['seq'=8,'fsdp'=4] {'seq'}, dimensions={2} | all-to-all | bytes 4194304 | tf_op jit(solution)/shard_map/all_to_all | solution.py:318
  1199.1 48.6 %reduce-scatter.11.cloned.1.call-done = bf16[256,2048]{1,0:T(8,128)(2,1)} async-done(((bf16[1024,2048]{1,0:T(8,128)(2,1)}), bf16[256,2048]{1,0:T(8,128)(2,1)}) %reduce-scatter.11.cloned.1.call-update) | async-done | bytes 1048592 | tf_op jit(solution)/shard_map/reduce_scatter | solution.py:330
  1249.6 8.0 all-gather.4
  1270.8 14.3 fusion.80
  1289.5 17.7 %fusion.68 = (f32[2048]{0:T(1024)S(1)}, f32[128]{0:T(128)S(1)}, f32[128]{0:T(128)S(1)}, f32[2048]{0:T(1024)S(1)}, f32[128,2048]{1,0:T(8,128)}) fusion(bf16[1,128,2048]{2,1,0:T(8,128)(2,1)S(1)} %copy-done.4, f32[128]{0:T(128)S(1)} %copy-done.23, f32[128]{0:T(128)S(1)} %copy-done.21, f32[2048]{0:T(1024)S(1)} %bitcast.281, f32[128,2048]{1,0:T(8,128)} %fusion.80, ...), kind=kOutput, calls=%fused_computation.96 | convolution fusion | flops 4297846784 | bytes 38299648 | tf_op jit(solution)/shard_map/dot_general | solution.py:45
  1310.6 43.6 %all-reduce.9 = (bf16[2048]{0:T(1024)(128)(2,1)S(1)}, bf16[2048]{0:T(1024)(128)(2,1)S(1)}, bf16[6144]{0:T(1024)(128)(2,1)S(1)}, bf16[2048]{0:T(1024)(128)(2,1)S(1)}, bf16[8192]{0:T(1024)(128)(2,1)S(1)}) all-reduce(f32[2048]{0:T(1024)S(1)} %reshape.440, ...), channel_id=3, replica_groups=mesh['seq'=8,'fsdp'=4] {'seq','fsdp'}, use_global_device_ids=true, to_apply=%region_12.13.clone | all-reduce | flops 20480 | bytes 122880
  1355.5 15.7 %all-reduce.10 = (bf16[512]{0:T(512)(128)(2,1)S(1)}, bf16[512]{0:T(512)(128)(2,1)S(1)}, bf16[1536]{0:T(1024)(128)(2,1)S(1)}, bf16[512]{0:T(512)(128)(2,1)S(1)}) all-reduce(bf16[512]{0:T(512)(128)(2,1)S(1)} %dynamic-update-slice, bf16[512]{0:T(512)(128)(2,1)S(1)} %dynamic-update-slice.1, ...), channel_id=1, replica_groups=mesh['seq'=8,'fsdp'=4] {'seq'}, use_global_device_ids=true, to_apply=%add | all-reduce | flops 3072 | bytes 12288
  1373.0 11.5 all-gather.6
  1385.2 14.4 fusion.53
  1399.6 9.3 convert_element_type.208
  1408.9 19.1 %all-gather.32.cloned.1.call-done = bf16[512,8192]{1,0:T(8,128)(2,1)} async-done(((bf16[512,1024]{1,0:T(8,128)(2,1)}), bf16[512,8192]{1,0:T(8,128)(2,1)}) %all-gather.32.cloned.1.call-update) | async-done | bytes 8388624 | tf_op jit(solution)/shard_map/all_gather | solution.py:348
  1428.0 12.5 convert_element_type.217
  1440.5 69.5 %all-gather.34.cloned.1.call-done = bf16[2048,2048]{1,0:T(8,128)(2,1)} async-done(((bf16[256,2048]{1,0:T(8,128)(2,1)}), bf16[2048,2048]{1,0:T(8,128)(2,1)}) %all-gather.34.cloned.1.call-update) | async-done | bytes 8388624 | tf_op jit(solution)/shard_map/all_gather | solution.py:351
  1510.0 11.7 convert_element_type.222
  (281 shorter events, 230.4 us)
Async XLA Ops:
  7.2 93.1 %all-gather.20.cloned.1.call-start = ((), (), s32[]{:S(2)}) async-start(), calls=%async_computation.13 | async-start | bytes 10485760 | tf_op jit(solution)/shard_map/all_gather | solution.py:158
  7.9 321.8 %all-gather.18.cloned.1.call-start = ((), (), s32[]{:S(2)}) async-start(), calls=%async_computation.12 | async-start | bytes 31457280 | tf_op jit(solution)/shard_map/all_gather | solution.py:157
  8.7 598.8 %all-gather.36.cloned.1.call-start = ((), (), s32[]{:S(2)}) async-start(), calls=%async_computation.25 | async-start | bytes 4718592 | tf_op jit(solution)/shard_map/all_gather | solution.py:290
  9.4 634.9 %all-gather.26.cloned.1.call-start = ((), (), s32[]{:S(2)}) async-start(), calls=%async_computation.16 | async-start | bytes 4718592 | tf_op jit(solution)/shard_map/all_gather | solution.py:289
  29.6 721.7 %all-gather.22.cloned.1.call-start = ((), (), s32[]{:S(2)}) async-start(), calls=%async_computation.14 | async-start | bytes 41943040 | tf_op jit(solution)/shard_map/all_gather | solution.py:159
  30.2 70.1 %copy-start.11 = (bf16[1,128,2048]{2,1,0:T(8,128)(2,1)S(1)}, bf16[1,128,2048]{2,1,0:T(8,128)(2,1)}, u32[]{:S(2)}) copy-start(bf16[1,128,2048]{2,1,0:T(8,128)(2,1)} %param.31) | copy-start | bytes 1572868
  30.2 1019.9 %all-gather.24.cloned.1.call-start = ((), (), s32[]{:S(2)}) async-start(), calls=%async_computation.15 | async-start | bytes 41943040 | tf_op jit(solution)/shard_map/all_gather | solution.py:160
  39.4 290.4 %copy-start.9 = (bf16[128,2048]{1,0:T(8,128)(2,1)S(1)}, bf16[128,2048]{1,0:T(8,128)(2,1)}, u32[]{:S(2)}) copy-start(bf16[128,2048]{1,0:T(8,128)(2,1)} %fusion.64) | copy-start | bytes 1572868
  107.4 240.2 %all-to-all-start.2 = ((bf16[128,8,256]{2,0,1:T(8,128)(2,1)}), bf16[128,8,256]{2,0,1:T(8,128)(2,1)}, u32[]{:S(2)}, u32[]{:S(2)}) async-start(bf16[128,8,256]{2,0,1:T(8,128)(2,1)} %bitcast.210), calls=%async_computation.2 | async-start | bytes 1048576 | tf_op jit(solution)/shard_map/all_to_all | solution.py:240
  347.6 63.0 %all-to-all-start = ((bf16[128,3,8,256]{0,3,1,2:T(8,128)(2,1)}), bf16[128,3,8,256]{0,3,1,2:T(8,128)(2,1)}, u32[]{:S(2)}, u32[]{:S(2)}) async-start(bf16[128,3,8,256]{0,3,1,2:T(8,128)(2,1)} %copy.106), calls=%async_computation | async-start | bytes 3145728 | tf_op jit(solution)/shard_map/all_to_all | solution.py:198
  457.1 71.6 %all-to-all-start.1 = ((bf16[8,2,16384]{2,1,0:T(2,128)(2,1)}), bf16[8,2,16384]{2,1,0:T(2,128)(2,1)}, u32[]{:S(2)}, u32[]{:S(2)}) async-start(bf16[8,2,16384]{2,1,0:T(2,128)(2,1)} %reshape.497), calls=%async_computation.1 | async-start | bytes 1048576 | tf_op jit(solution)/shard_map/all_to_all | solution.py:204
  528.8 54.0 %all-to-all-start.3 = ((bf16[1024,3,1,256]{3,1,2,0:T(4,128)(2,1)}), bf16[1024,3,1,256]{3,1,2,0:T(4,128)(2,1)S(1)}, u32[]{:S(2)}, u32[]{:S(2)}) async-start(bf16[1024,3,1,256]{3,1,2,0:T(4,128)(2,1)} %copy.114), calls=%async_computation.3 | async-start | bytes 4194304 | tf_op jit(solution)/shard_map/all_to_all | solution.py:256
  582.8 19.5 %all-to-all-start.5 = ((bf16[128,4,8,64]{0,3,1,2:T(8,128)(2,1)}), bf16[128,4,8,64]{0,3,1,2:T(8,128)(2,1)}, u32[]{:S(2)}, u32[]{:S(2)}) async-start(bf16[128,4,8,64]{0,3,1,2:T(8,128)(2,1)} %copy.122), calls=%async_computation.6 | async-start | bytes 1048576 | tf_op jit(solution)/shard_map/all_to_all | solution.py:311
  602.3 41.3 %all-to-all-start.4 = ((bf16[128,8,768]{0,2,1:T(8,128)(2,1)}), bf16[128,8,768]{0,2,1:T(8,128)(2,1)S(1)}, u32[]{:S(2)}, u32[]{:S(2)}) async-start(bf16[128,8,768]{0,2,1:T(8,128)(2,1)} %bitcast.37), calls=%async_computation.4 | async-start | bytes 3145728 | tf_op jit(solution)/shard_map/all_to_all | solution.py:293
  605.9 591.2 %reduce-scatter.7.cloned.1.call-start = ((), (), s32[]{:S(2)}) async-start(), calls=%async_computation.19 | async-start | bytes 1310720 | tf_op jit(solution)/shard_map/reduce_scatter | solution.py:330
  612.0 585.8 %reduce-scatter.5.cloned.1.call-start = ((), (), s32[]{:S(2)}) async-start(), calls=%async_computation.17 | async-start | bytes 3932160 | tf_op jit(solution)/shard_map/reduce_scatter | solution.py:330
  644.3 107.0 %copy-start.10 = (bf16[128,2048]{1,0:T(8,128)(2,1)S(1)}, bf16[128,2048]{1,0:T(8,128)(2,1)}, u32[]{:S(2)}) copy-start(bf16[128,2048]{1,0:T(8,128)(2,1)} %fusion.64) | copy-start | bytes 1572868
  651.8 398.3 %copy-start.12 = (bf16[1,128,2048]{2,1,0:T(8,128)(2,1)S(1)}, bf16[1,128,2048]{2,1,0:T(8,128)(2,1)}, u32[]{:S(2)}) copy-start(bf16[1,128,2048]{2,1,0:T(8,128)(2,1)} %param.31) | copy-start | bytes 1572868
  651.8 546.5 %reduce-scatter.9.cloned.1.call-start = ((), (), s32[]{:S(2)}) async-start(), calls=%async_computation.21 | async-start | bytes 5242880 | tf_op jit(solution)/shard_map/reduce_scatter | solution.py:330
  1068.1 53.9 %copy-start.31 = (bf16[1024,2048]{1,0:T(8,128)(2,1)S(1)}, bf16[1024,2048]{1,0:T(8,128)(2,1)}, u32[]{:S(2)}) copy-start(bf16[1024,2048]{1,0:T(8,128)(2,1)} %all-gather.26.cloned.1.call-done) | copy-start | bytes 12582916
  1128.3 119.4 %reduce-scatter.11.cloned.1.call-start = ((), (), s32[]{:S(2)}) async-start(), calls=%async_computation.23 | async-start | bytes 5242880 | tf_op jit(solution)/shard_map/reduce_scatter | solution.py:330
  1136.4 54.5 %copy-start.30 = (bf16[1,1024,2048]{2,1,0:T(8,128)(2,1)S(1)}, bf16[1,1024,2048]{2,1,0:T(8,128)(2,1)}, u32[]{:S(2)}) copy-start(bf16[1,1024,2048]{2,1,0:T(8,128)(2,1)} %all-gather.36.cloned.1.call-done) | copy-start | bytes 12582916
  1196.9 52.7 %copy-start.28 = (bf16[512]{0:T(512)(128)(2,1)S(1)}, bf16[512]{0:T(512)(128)(2,1)}, u32[]{:S(2)}) copy-start(bf16[512]{0:T(512)(128)(2,1)} %param.24) | copy-start | bytes 3076
  1196.9 60.7 %copy-start.29 = (bf16[512]{0:T(512)(128)(2,1)S(1)}, bf16[512]{0:T(512)(128)(2,1)}, u32[]{:S(2)}) copy-start(bf16[512]{0:T(512)(128)(2,1)} %param.28) | copy-start | bytes 3076
  1196.9 67.9 %copy-start.4 = (bf16[1,128,2048]{2,1,0:T(8,128)(2,1)S(1)}, bf16[1,128,2048]{2,1,0:T(8,128)(2,1)}, u32[]{:S(2)}) copy-start(bf16[1,128,2048]{2,1,0:T(8,128)(2,1)} %param.18) | copy-start | bytes 1572868
  1197.0 67.9 %copy-start.8 = (bf16[128,8,1,256]{0,3,1,2:T(8,128)(2,1)S(1)}, bf16[128,8,1,256]{0,3,1,2:T(8,128)(2,1)}, u32[]{:S(2)}) copy-start(bf16[128,8,1,256]{0,3,1,2:T(8,128)(2,1)} %copy-done.7) | copy-start | bytes 1572868
  1197.0 88.2 %all-gather.30.cloned.1.call-start = ((), (), s32[]{:S(2)}) async-start(), calls=%async_computation.20 | async-start | bytes 2359296 | tf_op jit(solution)/shard_map/all_gather | solution.py:345
  1197.7 201.9 %all-gather.28.cloned.1.call-start = ((), (), s32[]{:S(2)}) async-start(), calls=%async_computation.18 | async-start | bytes 7077888 | tf_op jit(solution)/shard_map/all_gather | solution.py:342
  1198.3 229.7 %all-gather.32.cloned.1.call-start = ((), (), s32[]{:S(2)}) async-start(), calls=%async_computation.22 | async-start | bytes 9437184 | tf_op jit(solution)/shard_map/all_gather | solution.py:348
  1199.1 310.9 %all-gather.34.cloned.1.call-start = ((), (), s32[]{:S(2)}) async-start(), calls=%async_computation.24 | async-start | bytes 9437184 | tf_op jit(solution)/shard_map/all_gather | solution.py:351
  1307.2 78.0 %copy-start.6 = (bf16[128,8192]{1,0:T(8,128)(2,1)S(1)}, bf16[128,8192]{1,0:T(8,128)(2,1)}, u32[]{:S(2)}) copy-start(bf16[128,8192]{1,0:T(8,128)(2,1)} %get-tuple-element.254) | copy-start | bytes 6291460
  1371.8 149.9 %copy-start.19 = (f32[512]{0:T(512)}, f32[512]{0:T(512)S(1)}, u32[]{:S(2)}) copy-start(f32[512]{0:T(512)S(1)} %convert_element_type.215) | copy-start | bytes 6148
  (30 other events, 277.4 us)
Sparse Core Ops, SparseCore 0:
  9.9 90.3 all-gather.19
  102.2 227.5 all-gather.17
  331.4 74.1 all-gather.35
  407.6 45.9 all-gather.25
  455.2 296.0 all-gather.21
  753.0 297.0 all-gather.23
  1053.6 27.9 reduce-scatter.6
  1085.1 43.8 reduce-scatter.4
  1132.6 52.5 reduce-scatter.8
  1197.1 50.5 reduce-scatter.10
  1249.3 29.1 all-gather.29
  1279.9 64.8 all-gather.27
  1346.4 81.4 all-gather.31
  1429.4 80.4 all-gather.33
where the time goes:
time: 1540 us; the launch traced here: 1530 us
  waiting for transfers between devices  930 us (60%)
  blocking collectives  227 us (15%)
  matrix products  184 us (12%)
  other arithmetic  69 us (4%)
  local copies, waits for them, and re-layouts  68.4 us (4%)
  starting transfers between devices  27.6 us (2%)
  between operations  16.1 us (1%)
    all_gather x1, waiting for transfers between devices, body(): lax.all_gather(fc2_weight, 'fsdp', axis=0, tiled=True)  280 us
    all_gather x1, waiting for transfers between devices, body(): lax.all_gather(qkv_weight, 'fsdp', axis=0, tiled=True)  218 us
    all_gather x1, waiting for transfers between devices, body(): lax.all_gather(fc1_weight, 'fsdp', axis=0, tiled=True)  99.4 us
    all_gather x1, waiting for transfers between devices, body(): lax.all_gather(piece_down.astype(jnp.bfloat16), 'seq', axis=0, tiled=True)  69.5 us
    all_gather x1, waiting for transfers between devices, body(): lax.all_gather(dense_weight, 'fsdp', axis=0, tiled=True)  60.9 us
    unnamed x2, blocking collectives  59.4 us
    all_to_all x1, waiting for transfers between devices, body(): lax.all_to_all(outgoing, 'seq', split_axis=2, concat_axis=0, tiled=True)  56.5 us
    dot_general x4, matrix products, contract_cols(): lax.dot_general(left_side, right_side, (((1,), (1,)), ((), ())), preferre...  56.2 us
  transfers between devices with their start and end apart: 20, of which 11 were waited for; matrix products, arithmetic and copies ran while one was open for 20% of the time, Pallas kernels for 0%

commit v1 on v0

--- a/solution.py
+++ b/solution.py
@@ -7,6 +7,18 @@
 HEAD = 64
 ROT = 32
 norm_epsilon = 1e-05
+
+
+def gather_by_bits(x, axis, dim):
+    ways, here = (lax.axis_size(axis), lax.axis_index(axis))
+    grown, reach = (x, 1)
+    while reach < ways:
+        theirs = lax.ppermute(grown, axis, [(d, d ^ reach) for d in range(ways)])
+        mine_first = jnp.concatenate([grown, theirs], axis=dim)
+        theirs_first = jnp.concatenate([theirs, grown], axis=dim)
+        grown = jnp.where(here & reach == 0, mine_first, theirs_first)
+        reach = 2 * reach
+    return grown
 
 
 def rotary_angles(pos_row, rot_width):
@@ -154,7 +166,7 @@
     seq_count = lax.axis_size("seq")
     shard_count = lax.axis_size("fsdp")
     gathered = (
-        lax.all_gather(qkv_weight, "fsdp", axis=0, tiled=True),
+        gather_by_bits(qkv_weight, "fsdp", 0),
         lax.all_gather(dense_weight, "fsdp", axis=0, tiled=True),
         lax.all_gather(fc1_weight, "fsdp", axis=0, tiled=True),
         lax.all_gather(fc2_weight, "fsdp", axis=0, tiled=True),

time: 1540 us -> 1810 us (1.18)
  blocking collectives: 227 us -> 722 us
  waiting for transfers between devices: 930 us -> 675 us
  other arithmetic: 69 us -> 88.4 us
    all_gather x1, blocking collectives: 7.71 us -> 508 us  [body(): lax.all_gather(qkv_bias, 'fsdp', axis=0, tiled=True)]
    all_gather x1, waiting for transfers between devices: 280 us -> 0.01 us  [body(): lax.all_gather(fc2_weight, 'fsdp', axis=0, tiled=True)]
    ppermute x0 -> x2, waiting for transfers between devices: none -> 192 us  [gather_by_bits(): theirs = lax.ppermute(grown, axis, [(d, d ^ reach) for d in range(ways)])]
    all_gather x1, waiting for transfers between devices: 99.4 us -> 0.02 us  [body(): lax.all_gather(fc1_weight, 'fsdp', axis=0, tiled=True)]
    all_gather x1, waiting for transfers between devices: 60.9 us -> 0.01 us  [body(): lax.all_gather(dense_weight, 'fsdp', axis=0, tiled=True)]
    all_gather x1, waiting for transfers between devices: 0.01 us -> 52 us  [body(): lax.all_gather(piece_qkv.astype(jnp.bfloat16), 'seq', axis=1, tiled=True)]
    all_gather x1, waiting for transfers between devices: 69.5 us -> 35.8 us  [body(): lax.all_gather(piece_down.astype(jnp.bfloat16), 'seq', axis=0, tiled=True)]
    all_to_all x1, waiting for transfers between devices: 56.5 us -> 36 us  [body(): lax.all_to_all(outgoing, 'seq', split_axis=2, concat_axis=0, tiled=True)]
  transfers between devices with their start and end apart: 20 -> 22, of which waited for: 11 -> 10; matrix products, arithmetic and copies ran while one was open for 20% -> 18% of each run, Pallas kernels for 0% -> 0%
where the time goes in v1:
time: 1810 us; the launch traced here: 1800 us
  blocking collectives  722 us (40%)
  waiting for transfers between devices  675 us (37%)
  matrix products  187 us (10%)
  other arithmetic  88.4 us (5%)
  local copies, waits for them, and re-layouts  72 us (4%)
  starting transfers between devices  29.9 us (2%)
    all_gather x1, blocking collectives, body(): lax.all_gather(qkv_bias, 'fsdp', axis=0, tiled=True)  508 us
    all_gather x1, waiting for transfers between devices, body(): lax.all_gather(qkv_weight, 'fsdp', axis=0, tiled=True)  225 us
    ppermute x2, waiting for transfers between devices, gather_by_bits(): theirs = lax.ppermute(grown, axis, [(d, d ^ reach) for d in range(ways)])  192 us
    unnamed x2, blocking collectives  59.4 us
    dot_general x4, matrix products, contract_cols(): lax.dot_general(left_side, right_side, (((1,), (1,)), ((), ())), preferre...  56.7 us
    all_to_all x1, blocking collectives, body(): lax.all_to_all(activated.reshape(tok_len, shard_count, seq_count, row_dow...  52.8 us
    all_gather x1, waiting for transfers between devices, body(): lax.all_gather(piece_qkv.astype(jnp.bfloat16), 'seq', axis=1, tiled=True)  52 us
    all_to_all x1, blocking collectives, body(): lax.all_to_all(grad_pre.reshape(tok_len, seq_count, col_up), 'seq', split...  51.7 us
  transfers between devices with their start and end apart: 22, of which 10 were waited for; matrix products, arithmetic and copies ran while one was open for 18% of the time, Pallas kernels for 0%

profile of v1, /device:TPU:0, one launch (start us, length us, event | category | flops | bytes accessed | tf_op | source)
XLA Modules:
  0.0 1797.9 jit_solution(5753024446363257602)
XLA Ops:
  9.4 9.6 all-gather.1
  19.7 8.3 all-gather.2
  35.0 191.6 %collective-permute-done = bf16[512,6144]{1,0:T(8,128)(2,1)} collective-permute-done((bf16[512,6144]{1,0:T(8,128)(2,1)}, bf16[512,6144]{1,0:T(8,128)(2,1)}, u32[]{:S(2)}, u32[]{:S(2)}) %collective-permute-start) | collective-permute-done | bytes 6291488 | tf_op jit(solution)/shard_map/ppermute | solution.py:16
  226.7 15.9 maximum_select_fusion.2
  244.0 508.4 %all-gather.3 = bf16[4,1,1536]{2,1,0:T(2,128)(2,1)S(1)} all-gather(bf16[1,1,1536]{2,1,0:T(2,128)(2,1)S(1)} %reshape.474), channel_id=1, replica_groups=mesh['seq'=8,'fsdp'=4] {'fsdp'}, dimensions={0}, use_global_device_ids=true | all-gather | bytes 15360 | tf_op jit(solution)/shard_map/all_gather | solution.py:175
  764.7 20.0 %fusion.40 = f32[128,6144]{1,0:T(8,128)} fusion(bf16[128,2048]{1,0:T(8,128)(2,1)S(1)} %copy-done.11, bf16[1024,6144]{1,0:T(8,128)(2,1)} %collective-permute-done.1, bf16[1024,6144]{1,0:T(8,128)(2,1)} %maximum_select_fusion.2, pred[]{:T(512)S(6)} %eq.44, f32[6144]{0:T(1024)S(1)} %bitcast.292), kind=kOutput, calls=%fused_computation.53 | convolution fusion | flops 3335258112 | bytes 28860416 | tf_op jit(solution)/shard_map/dot_general | solution.py:201
  796.4 36.0 %all-to-all-done = bf16[128,3,8,256]{0,3,1,2:T(8,128)(2,1)} async-done(((bf16[128,3,8,256]{0,3,1,2:T(8,128)(2,1)}), bf16[128,3,8,256]{0,3,1,2:T(8,128)(2,1)}, u32[]{:S(2)}, u32[]{:S(2)}) %all-to-all-start) | async-done | bytes 1572896 | tf_op jit(solution)/shard_map/all_to_all | solution.py:210
  843.0 20.8 %while.27 = (s32[]{:T(128)}, bf16[2,512,4,64]{1,3,2,0:T(8,128)(2,1)}, f32[2,4,512]{2,1,0:T(4,128)S(1)}, s32[2]{0:T(128)S(1)}, s32[1024]{0:T(1024)S(1)}, /*index=...) while((s32[]{:T(128)}, ...), condition=%wide.region_5.6_spmd, body=%wide.region_2.5_spmd.sunk | while | flops 563608064 | bytes 31275748 | solution.py:100
  884.4 62.4 %while.28 = (s32[]{:T(128)}, f32[1024,4,64]{0,2,1:T(8,128)S(1)}, f32[1024,4,64]{0,2,1:T(8,128)S(1)}, bf16[2,512,4,64]{1,3,2,0:T(8,128)(2,1)}, s32[2]{0:T(128)S(1...) while((s32[]{:T(128)}, f32[1024,4,64]{0,2,1:T(8,128)S(1)}, ...), condition=%wide.region_8.9_spmd.clone, body=%wide.region_6.8_spmd.clone.sunk | while | flops 1366161920 | bytes 180411312 | solution.py:144
  962.0 43.7 %all-to-all-done.3 = bf16[1024,3,1,256]{3,1,2,0:T(4,128)(2,1)S(1)} async-done(((bf16[1024,3,1,256]{3,1,2,0:T(4,128)(2,1)}), bf16[1024,3,1,256]{3,1,2,0:T(4,128)(2,1)S(1)}, u32[]{:S(2)}, u32[]{:S(2)}) %all-to-all-start.3) | async-done | bytes 1572896 | tf_op jit(solution)/shard_map/all_to_all | solution.py:268
  1034.8 7.8 all_gather.73
  1042.6 24.0 %all-to-all-done.4 = bf16[128,8,768]{0,2,1:T(8,128)(2,1)S(1)} async-done(((bf16[128,8,768]{0,2,1:T(8,128)(2,1)}), bf16[128,8,768]{0,2,1:T(8,128)(2,1)S(1)}, u32[]{:S(2)}, u32[]{:S(2)}) %all-to-all-start.4) | async-done | bytes 1572896 | tf_op jit(solution)/shard_map/all_to_all | solution.py:305
  1067.3 7.4 convolution_convert_fusion.1
  1075.0 16.4 multiply_convert_fusion.1
  1091.4 18.2 %convert_reduce_fusion = (f32[8192]{0:T(1024)S(1)}, bf16[128,8192]{1,0:T(8,128)(2,1)S(1)}) fusion(f32[128,8192]{1,0:T(8,128)} %get-tuple-element.255, bf16[8192,2048]{1,0:T(8,128)(2,1)} %all-gather.22.cloned.1.call-done, bf16[1,128,2048]{2,1,0:T(8,128)(2,1)S(1)} %copy-done.9), kind=kOutput, calls=%fused_computation.67 | convolution fusion | flops 4318027776 | bytes 40402944 | tf_op jit(solution)/shard_map/dot_general | solution.py:57
  1109.8 51.7 %all_to_all.114 = bf16[128,8,1024]{2,0,1:T(8,128)(2,1)S(1)} all-to-all(bf16[128,8,1024]{2,0,1:T(8,128)(2,1)S(1)} %bitcast.255), channel_id=1, replica_groups=mesh['seq'=8,'fsdp'=4] {'seq'}, dimensions={1} | all-to-all | bytes 4194304 | tf_op jit(solution)/shard_map/all_to_all | solution.py:312
  1175.9 52.8 %all_to_all.115 = bf16[128,4,8,256]{0,3,1,2:T(8,128)(2,1)S(1)} all-to-all(bf16[128,4,8,256]{0,3,1,2:T(8,128)(2,1)} %copy.127), channel_id=1, replica_groups=mesh['seq'=8,'fsdp'=4] {'seq'}, dimensions={2} | all-to-all | bytes 4194304 | tf_op jit(solution)/shard_map/all_to_all | solution.py:330
  1238.9 48.5 %reduce-scatter.11.cloned.1.call-done = bf16[256,2048]{1,0:T(8,128)(2,1)} async-done(((bf16[1024,2048]{1,0:T(8,128)(2,1)}), bf16[256,2048]{1,0:T(8,128)(2,1)}) %reduce-scatter.11.cloned.1.call-update) | async-done | bytes 1048592 | tf_op jit(solution)/shard_map/reduce_scatter | solution.py:342
  1289.4 8.1 all-gather.4
  1297.5 7.3 all-gather.5
  1322.2 224.7 %all-gather.24.cloned.1.call-done = bf16[2048,6144]{1,0:T(8,128)(2,1)} async-done(((bf16[512,6144]{1,0:T(8,128)(2,1)}), bf16[2048,6144]{1,0:T(8,128)(2,1)}) %all-gather.24.cloned.1.call-update) | async-done | bytes 25165840 | tf_op jit(solution)/shard_map/all_gather | solution.py:234
  1547.0 14.2 fusion.89
  1561.2 52.0 %all-gather.28.cloned.1.call-done = bf16[512,6144]{1,0:T(8,128)(2,1)} async-done(((bf16[512,768]{1,0:T(8,128)(2,1)}), bf16[512,6144]{1,0:T(8,128)(2,1)}) %all-gather.28.cloned.1.call-update) | async-done | bytes 6291472 | tf_op jit(solution)/shard_map/all_gather | solution.py:354
  1613.2 9.7 convert_element_type.208
  1622.9 18.0 %fusion.76 = (f32[2048]{0:T(1024)S(1)}, f32[128]{0:T(128)S(1)}, f32[128]{0:T(128)S(1)}, f32[2048]{0:T(1024)S(1)}, f32[128,2048]{1,0:T(8,128)}) fusion(bf16[1,128,2048]{2,1,0:T(8,128)(2,1)S(1)} %copy-done.3, f32[128]{0:T(128)S(1)} %copy-done.22, f32[128]{0:T(128)S(1)} %copy-done.20, f32[2048]{0:T(1024)S(1)} %bitcast.280, f32[128,2048]{1,0:T(8,128)} %fusion.89, ...), kind=kOutput, calls=%fused_computation.105 | convolution fusion | flops 4297846784 | bytes 38299648 | tf_op jit(solution)/shard_map/dot_general | solution.py:57
  1644.4 44.4 %all-reduce.9 = (bf16[2048]{0:T(1024)(128)(2,1)S(1)}, bf16[2048]{0:T(1024)(128)(2,1)S(1)}, bf16[6144]{0:T(1024)(128)(2,1)S(1)}, bf16[2048]{0:T(1024)(128)(2,1)S(1)}, bf16[8192]{0:T(1024)(128)(2,1)S(1)}) all-reduce(f32[2048]{0:T(1024)S(1)} %reshape.440, ...), channel_id=3, replica_groups=mesh['seq'=8,'fsdp'=4] {'seq','fsdp'}, use_global_device_ids=true, to_apply=%region_12.13.clone | all-reduce | flops 20480 | bytes 122880
  1690.1 15.0 all-reduce.10
  1706.9 9.2 all-gather.6
  1716.7 14.4 fusion.61
  1731.1 11.8 convert_element_type.217
  1742.9 35.8 %all-gather.34.cloned.1.call-done = bf16[2048,2048]{1,0:T(8,128)(2,1)} async-done(((bf16[256,2048]{1,0:T(8,128)(2,1)}), bf16[2048,2048]{1,0:T(8,128)(2,1)}) %all-gather.34.cloned.1.call-update) | async-done | bytes 8388624 | tf_op jit(solution)/shard_map/all_gather | solution.py:363
  1778.6 11.7 convert_element_type.222
  (280 shorter events, 238.2 us)
Async XLA Ops:
  7.2 746.0 %all-gather.18.cloned.1.call-start = ((), (), s32[]{:S(2)}) async-start(), calls=%async_computation.12 | async-start | bytes 10485760 | tf_op jit(solution)/shard_map/all_gather | solution.py:170
  7.9 1022.4 %all-gather.36.cloned.1.call-start = ((), (), s32[]{:S(2)}) async-start(), calls=%async_computation.25 | async-start | bytes 4718592 | tf_op jit(solution)/shard_map/all_gather | solution.py:302
  8.7 1058.6 %all-gather.26.cloned.1.call-start = ((), (), s32[]{:S(2)}) async-start(), calls=%async_computation.16 | async-start | bytes 4718592 | tf_op jit(solution)/shard_map/all_gather | solution.py:301
  33.3 1041.7 %all-gather.20.cloned.1.call-start = ((), (), s32[]{:S(2)}) async-start(), calls=%async_computation.13 | async-start | bytes 41943040 | tf_op jit(solution)/shard_map/all_gather | solution.py:171
  33.9 1057.6 %all-gather.22.cloned.1.call-start = ((), (), s32[]{:S(2)}) async-start(), calls=%async_computation.14 | async-start | bytes 41943040 | tf_op jit(solution)/shard_map/all_gather | solution.py:172
  34.4 192.2 %collective-permute-start = (bf16[512,6144]{1,0:T(8,128)(2,1)}, bf16[512,6144]{1,0:T(8,128)(2,1)}, u32[]{:S(2)}, u32[]{:S(2)}) collective-permute-start(bf16[512,6144]{1,0:T(8,128)(2,1)} %param.21), channel_id=1, source_target_pairs={{0,1},{1,0},{2,3},{3,2},{4,5},{5,4},{6,7},{7,6},{8,9},{9,8},{10,11... | collective-permute-start | bytes 18874376 | tf_op jit(solution)/shard_map/ppermute | solution.py:16
  35.0 209.0 %copy-start.24 = (bf16[1536]{0:T(1024)(128)(2,1)S(1)}, bf16[1536]{0:T(1024)(128)(2,1)}, u32[]{:S(2)}) copy-start(bf16[1536]{0:T(1024)(128)(2,1)} %param.22) | copy-start | bytes 9220
  35.0 717.4 %copy-start.29 = (s32[1,128]{1,0:T(1,128)S(1)}, s32[1,128]{1,0:T(1,128)}, u32[]{:S(2)}) copy-start(s32[1,128]{1,0:T(1,128)} %param.30) | copy-start | bytes 1540
  35.0 718.2 %copy-start.8 = (bf16[1,128,2048]{2,1,0:T(8,128)(2,1)S(1)}, bf16[1,128,2048]{2,1,0:T(8,128)(2,1)}, u32[]{:S(2)}) copy-start(bf16[1,128,2048]{2,1,0:T(8,128)(2,1)} %param.31) | copy-start | bytes 1572868
  242.5 522.2 %collective-permute-start.1 = (bf16[1024,6144]{1,0:T(8,128)(2,1)}, bf16[1024,6144]{1,0:T(8,128)(2,1)}, u32[]{:S(2)}, u32[]{:S(2)}) collective-permute-start(bf16[1024,6144]{1,0:T(8,128)(2,1)} %maximum_select_fusion.2), channel_id=1, source_target_pairs={{0,2},{1,3},{2,0},{3,1},{4,6},{5,7},{6,4},{7,5},{8,10},{9,11},{10,... | collective-permute-start | bytes 37748744 | tf_op jit(solution)/shard_map/ppermute | solution.py:16
  760.3 28.9 %all-to-all-start.2 = ((bf16[128,8,256]{2,0,1:T(8,128)(2,1)}), bf16[128,8,256]{2,0,1:T(8,128)(2,1)}, u32[]{:S(2)}, u32[]{:S(2)}) async-start(bf16[128,8,256]{2,0,1:T(8,128)(2,1)} %bitcast.209), calls=%async_computation.2 | async-start | bytes 1048576 | tf_op jit(solution)/shard_map/all_to_all | solution.py:252
  789.2 43.2 %all-to-all-start = ((bf16[128,3,8,256]{0,3,1,2:T(8,128)(2,1)}), bf16[128,3,8,256]{0,3,1,2:T(8,128)(2,1)}, u32[]{:S(2)}, u32[]{:S(2)}) async-start(bf16[128,3,8,256]{0,3,1,2:T(8,128)(2,1)} %copy.106), calls=%async_computation | async-start | bytes 3145728 | tf_op jit(solution)/shard_map/all_to_all | solution.py:210
  879.0 72.7 %all-to-all-start.1 = ((bf16[8,2,16384]{2,1,0:T(2,128)(2,1)}), bf16[8,2,16384]{2,1,0:T(2,128)(2,1)}, u32[]{:S(2)}, u32[]{:S(2)}) async-start(bf16[8,2,16384]{2,1,0:T(2,128)(2,1)} %reshape.497), calls=%async_computation.1 | async-start | bytes 1048576 | tf_op jit(solution)/shard_map/all_to_all | solution.py:216
  951.7 54.1 %all-to-all-start.3 = ((bf16[1024,3,1,256]{3,1,2,0:T(4,128)(2,1)}), bf16[1024,3,1,256]{3,1,2,0:T(4,128)(2,1)S(1)}, u32[]{:S(2)}, u32[]{:S(2)}) async-start(bf16[1024,3,1,256]{3,1,2,0:T(4,128)(2,1)} %copy.114), calls=%async_computation.3 | async-start | bytes 4194304 | tf_op jit(solution)/shard_map/all_to_all | solution.py:268
  1005.7 19.5 %all-to-all-start.5 = ((bf16[128,4,8,64]{0,3,1,2:T(8,128)(2,1)}), bf16[128,4,8,64]{0,3,1,2:T(8,128)(2,1)}, u32[]{:S(2)}, u32[]{:S(2)}) async-start(bf16[128,4,8,64]{0,3,1,2:T(8,128)(2,1)} %copy.122), calls=%async_computation.6 | async-start | bytes 1048576 | tf_op jit(solution)/shard_map/all_to_all | solution.py:323
  1025.2 41.3 %all-to-all-start.4 = ((bf16[128,8,768]{0,2,1:T(8,128)(2,1)}), bf16[128,8,768]{0,2,1:T(8,128)(2,1)S(1)}, u32[]{:S(2)}, u32[]{:S(2)}) async-start(bf16[128,8,768]{0,2,1:T(8,128)(2,1)} %bitcast.37), calls=%async_computation.4 | async-start | bytes 3145728 | tf_op jit(solution)/shard_map/all_to_all | solution.py:305
  1028.8 207.4 %reduce-scatter.7.cloned.1.call-start = ((), (), s32[]{:S(2)}) async-start(), calls=%async_computation.19 | async-start | bytes 1310720 | tf_op jit(solution)/shard_map/reduce_scatter | solution.py:342
  1034.7 202.9 %reduce-scatter.5.cloned.1.call-start = ((), (), s32[]{:S(2)}) async-start(), calls=%async_computation.17 | async-start | bytes 3932160 | tf_op jit(solution)/shard_map/reduce_scatter | solution.py:342
  1074.8 163.5 %reduce-scatter.9.cloned.1.call-start = ((), (), s32[]{:S(2)}) async-start(), calls=%async_computation.21 | async-start | bytes 5242880 | tf_op jit(solution)/shard_map/reduce_scatter | solution.py:342
  1167.8 119.7 %reduce-scatter.11.cloned.1.call-start = ((), (), s32[]{:S(2)}) async-start(), calls=%async_computation.23 | async-start | bytes 5242880 | tf_op jit(solution)/shard_map/reduce_scatter | solution.py:342
  1236.2 81.9 %all-gather.30.cloned.1.call-start = ((), (), s32[]{:S(2)}) async-start(), calls=%async_computation.20 | async-start | bytes 2359296 | tf_op jit(solution)/shard_map/all_gather | solution.py:357
  1236.8 68.0 %copy-start.3 = (bf16[1,128,2048]{2,1,0:T(8,128)(2,1)S(1)}, bf16[1,128,2048]{2,1,0:T(8,128)(2,1)}, u32[]{:S(2)}) copy-start(bf16[1,128,2048]{2,1,0:T(8,128)(2,1)} %param.18) | copy-start | bytes 1572868
  1236.8 68.0 %copy-start.7 = (bf16[128,8,1,256]{0,3,1,2:T(8,128)(2,1)S(1)}, bf16[128,8,1,256]{0,3,1,2:T(8,128)(2,1)}, u32[]{:S(2)}) copy-start(bf16[128,8,1,256]{0,3,1,2:T(8,128)(2,1)} %copy-done.6) | copy-start | bytes 1572868
  1236.8 310.1 %all-gather.24.cloned.1.call-start = ((), (), s32[]{:S(2)}) async-start(), calls=%async_computation.15 | async-start | bytes 31457280 | tf_op jit(solution)/shard_map/all_gather | solution.py:234
  1237.6 375.6 %all-gather.28.cloned.1.call-start = ((), (), s32[]{:S(2)}) async-start(), calls=%async_computation.18 | async-start | bytes 7077888 | tf_op jit(solution)/shard_map/all_gather | solution.py:354
  1238.2 492.9 %all-gather.32.cloned.1.call-start = ((), (), s32[]{:S(2)}) async-start(), calls=%async_computation.22 | async-start | bytes 9437184 | tf_op jit(solution)/shard_map/all_gather | solution.py:360
  1238.9 539.7 %all-gather.34.cloned.1.call-start = ((), (), s32[]{:S(2)}) async-start(), calls=%async_computation.24 | async-start | bytes 9437184 | tf_op jit(solution)/shard_map/all_gather | solution.py:363
  1561.2 61.7 %copy-start.15 = (f32[4,1,512]{2,1,0:T(1,128)S(1)}, f32[4,1,512]{2,1,0:T(1,128)}, u32[]{:S(2)}) copy-start(f32[4,1,512]{2,1,0:T(1,128)} %copy-done.14) | copy-start | bytes 24580
  1561.2 61.7 %copy-start.20 = (f32[128]{0:T(128)S(1)}, f32[128]{0:T(128)}, u32[]{:S(2)}) copy-start(f32[128]{0:T(128)} %copy-done.19) | copy-start | bytes 1540
  1561.2 61.7 %copy-start.22 = (f32[128]{0:T(128)S(1)}, f32[128]{0:T(128)}, u32[]{:S(2)}) copy-start(f32[128]{0:T(128)} %copy-done.21) | copy-start | bytes 1540
  1641.0 75.7 %copy-start.5 = (bf16[128,8192]{1,0:T(8,128)(2,1)S(1)}, bf16[128,8192]{1,0:T(8,128)(2,1)}, u32[]{:S(2)}) copy-start(bf16[128,8192]{1,0:T(8,128)(2,1)} %get-tuple-element.254) | copy-start | bytes 6291460
  1705.6 84.7 %copy-start.18 = (f32[512]{0:T(512)}, f32[512]{0:T(512)S(1)}, u32[]{:S(2)}) copy-start(f32[512]{0:T(512)S(1)} %convert_element_type.215) | copy-start | bytes 6148
  (29 other events, 484.9 us)
Sparse Core Ops, SparseCore 0:
  9.8 147.7 all-gather.17
  159.2 46.8 all-gather.35
  208.3 45.6 all-gather.25
  255.7 527.8 all-gather.19
  785.2 297.2 all-gather.21
  1085.9 27.9 reduce-scatter.6
  1117.4 43.8 reduce-scatter.4
  1167.9 50.9 reduce-scatter.8
  1236.3 51.1 reduce-scatter.10
  1288.9 29.1 all-gather.29
  1320.0 226.9 all-gather.23
  1548.4 64.6 all-gather.27
  1614.8 81.7 all-gather.31
  1698.0 80.5 all-gather.33
